TPU v7x, 32 devices: a whole 2x2x4 slice. The times are simulated.
32 devices in a mesh: rep: 1, dp: 32 (over x, y, z, core).
Axes of the slice: x: 2, y: 2, z: 4, core: 2. Of those that a mesh axis runs over, the one named last changes fastest.
Arguments:
- a: bfloat16 [32, 2, 8192, 640], P(('rep', 'dp'))
- g: bfloat16 [32, 2, 8192, 4096], P(('rep', 'dp'))
Outputs:
- output: bfloat16 [2, 640, 4096], P('rep')
All inputs are finite; a program needn't handle non-finite values.
Results may differ from a plain program's by a relative error of at most 0.012.
Values are sent between devices in bfloat16 or wider.
A program may use at most 2 GiB of HBM per device.

v0:
```python
import jax
import jax.numpy as jnp


def solution(mesh):
    groups = mesh.shape["rep"]

    def step(a, g):
        a, g = (t.reshape(groups, -1, *t.shape[1:]) for t in (a, g))
        sums = jnp.einsum("rsntd,rsntf->rndf", a, g, preferred_element_type=jnp.float32)
        return sums.astype(jnp.bfloat16).reshape(-1, *sums.shape[2:])

    return step
```

profile of v0, /device:TPU:0, one launch (start us, length us, event | category | flops | bytes accessed | tf_op | source)
XLA Modules:
  0.0 442.8 jit_solution(4550897302848930717)
XLA Ops:
  0.0 101.2 %fusion = f32[2,640,4096]{2,1,0:T(8,128)} fusion(bf16[1,2,8192,4096]{3,2,1,0:T(8,128)(2,1)} %param.1, bf16[1,2,8192,640]{3,2,1,0:T(8,128)(2,1)} %param), kind=kOutput, calls=%fused_computation | convolution fusion | flops 85899345920 | bytes 176160768 | tf_op jit(solution)/rsntd,rsntf->rndf/dot_general | solution.py:10
  101.2 341.5 %all-reduce.2 = bf16[2,640,4096]{2,1,0:T(8,128)(2,1)} all-reduce(f32[2,640,4096]{2,1,0:T(8,128)} %fusion), channel_id=1, replica_groups=mesh['axis_0'=32] {'axis_0'}, use_global_device_ids=true, to_apply=%add.clone | all-reduce | flops 5242880 | bytes 31457280 | tf_op jit(solution)/rsntd,rsntf->rndf/dot_general | solution.py:10
where the time goes:
time: 443 us
  blocking collectives  342 us (77%)
  matrix products  101 us (23%)
    dot_general x1, blocking collectives, step(): jnp.einsum('rsntd,rsntf->rndf', a, g, preferred_element_type=jnp.float32)  342 us
    dot_general x1, matrix products, step(): jnp.einsum('rsntd,rsntf->rndf', a, g, preferred_element_type=jnp.float32)  101 us

commit v1 on v0

v1 whole, which is shorter than its diff:
```python
import jax
import jax.numpy as jnp
from jax import lax
from jax.experimental import pallas as pl
from jax.experimental.pallas import tpu as pltpu
from jax.sharding import PartitionSpec as P

T, D, FF, MATS = 8192, 640, 4096, 2
FC = 1024
TK = 2048
KS = T // TK
PER = FF // FC
NC = MATS * PER
NG = 3
PR = D // 16
GROUPS = (("xyw", 384), ("yxw", 384), ("wxy", 128), ("wyx", 128))
OFFSETS = (4, 5, 8, 10, 12, 15, 17, 19, 22, 23)
RS_LO = (0, 8, 12, 14, 15)
RS_N = (8, 4, 2, 1, 1)
F32, BF16 = jnp.float32, jnp.bfloat16


def kernel(a_ref, g_ref, o_ref, ab, gb, acc, *rest):
    ng = len(GROUPS)
    part, send, recv, done = (rest[i * ng:(i + 1) * ng] for i in range(4))
    asem, gsem, rs_s, rs_r, ag_s, ag_r, osem = rest[4 * ng:]
    me = lax.axis_index("dp")
    bits = {"x": me // 16, "y": (me // 8) % 2, "h": (me // 4) % 2, "w": (me // 2) % 2, "c": me % 2}
    size = {"x": 16, "y": 8, "h": 4, "w": 2, "c": 1}
    peer = {d: me + size[d] * (1 - 2 * bits[d]) for d in bits}

    def a_copy(n, k):
        rows = pl.ds(k * TK, TK)
        return pltpu.make_async_copy(a_ref.at[0, n, rows, :], ab.at[k], asem.at[k])

    def g_copy(t):
        c, k = t // KS, t % KS
        rows = pl.ds(pl.multiple_of(k * TK, TK), TK)
        cols = pl.ds(pl.multiple_of((c % PER) * FC, FC), FC)
        return pltpu.make_async_copy(g_ref.at[0, c // PER, rows, cols], gb.at[t % NG], gsem.at[t % NG])

    for k in range(KS):
        a_copy(0, k).start()
        if k < NG - 1:
            g_copy(jnp.int32(k)).start()

    barrier = pltpu.get_barrier_semaphore()
    for d in peer:
        pl.semaphore_signal(barrier, inc=1, device_id=(0, peer[d]), device_id_type=pl.DeviceIdType.MESH)
    pl.semaphore_wait(barrier, len(peer))

    def b(gi, j):
        return bits[GROUPS[gi][0][j]]

    def rs_copy(gi, ph, c):
        d = "c" if ph == 0 else "h" if ph == 4 else GROUPS[gi][0][ph - 1]
        par, where = c % 2, pl.ds(RS_LO[ph], RS_N[ph])
        return pltpu.make_async_remote_copy(
            src_ref=send[gi].at[par, where], dst_ref=recv[gi].at[par, where],
            send_sem=rs_s.at[gi, ph, par], recv_sem=rs_r.at[gi, ph, par],
            device_id=(0, peer[d]), device_id_type=pl.DeviceIdType.MESH)

    def ag_copy(gi, ph, c):
        d = "c" if ph == 3 else GROUPS[gi][0][2 - ph]
        n = 1 << ph
        first = bits["c"] * 8 if ph < 4 else 0
        for j in range(3 - ph):
            first = first + b(gi, j) * (4 >> j)
        where = pl.ds(first, n)
        return pltpu.make_async_remote_copy(
            src_ref=done[gi].at[c, where], dst_ref=done[gi].at[c, where],
            send_sem=ag_s.at[gi, ph, c], recv_sem=ag_r.at[gi, ph, c],
            device_id=(0, peer[d]), device_id_type=pl.DeviceIdType.MESH)

    def out_copy(gi, c):
        off = sum(w for _, w in GROUPS[:gi])
        cols = pl.ds(pl.multiple_of((c % PER) * FC + off, 128), GROUPS[gi][1])
        return pltpu.make_async_copy(done[gi].at[c], o_ref.at[c // PER, :, :, cols], osem.at[gi, c])

    def rows_of(piece):
        return pl.ds(pl.multiple_of(piece * PR, 8), PR)

    def stage(s, c):
        par = c % 2
        for gi, (_, w) in enumerate(GROUPS):
            off = sum(v for _, v in GROUPS[:gi])
            cols = slice(off, off + w)
            if s == 0:
                other = (1 - bits["c"]) * 8
                for j in range(8):
                    send[gi][par, j] = acc[par, rows_of(other + j), cols].astype(BF16)
                rs_copy(gi, 0, c).start()
            elif s == 1:
                rs_copy(gi, 0, c).wait()
                own = bits["c"] * 8
                keep, give = b(gi, 0) * 4, (1 - b(gi, 0)) * 4
                for j in range(4):
                    send[gi][par, 8 + j] = (acc[par, rows_of(own + give + j), cols]
                                            + recv[gi][par, give + j].astype(F32)).astype(BF16)
                rs_copy(gi, 1, c).start()
                for j in range(4):
                    part[gi][par, j] = (acc[par, rows_of(own + keep + j), cols]
                                        + recv[gi][par, keep + j].astype(F32))
            elif s in (2, 3):
                rs_copy(gi, s - 1, c).wait()
                n = 2 if s == 2 else 1
                base = 0 if s == 2 else b(gi, 1) * 2
                keep, give = b(gi, s - 1) * n, (1 - b(gi, s - 1)) * n
                lo = RS_LO[s - 1]
                for j in range(n):
                    send[gi][par, RS_LO[s] + j] = (part[gi][par, base + give + j]
                                                   + recv[gi][par, lo + give + j].astype(F32)).astype(BF16)
                rs_copy(gi, s, c).start()
                for j in range(n):
                    part[gi][par, base + keep + j] = (part[gi][par, base + keep + j]
                                                      + recv[gi][par, lo + keep + j].astype(F32))
            elif s == 4:
                rs_copy(gi, 3, c).wait()
                mine = b(gi, 1) * 2 + b(gi, 2)
                send[gi][par, 15] = (part[gi][par, mine] + recv[gi][par, 14].astype(F32)).astype(BF16)
                rs_copy(gi, 4, c).start()
            elif s == 5:
                rs_copy(gi, 4, c).wait()
                mine = bits["c"] * 8 + b(gi, 0) * 4 + b(gi, 1) * 2 + b(gi, 2)
                done[gi][c, mine] = (send[gi][par, 15].astype(F32) + recv[gi][par, 15].astype(F32)).astype(BF16)
                ag_copy(gi, 0, c).start()
            elif s in (6, 7, 8):
                ag_copy(gi, s - 6, c).wait()
                ag_copy(gi, s - 5, c).start()
            else:
                ag_copy(gi, 3, c).wait()
                out_copy(gi, c).start()

    def dot(k, slot):
        return lax.dot_general(ab[k], gb[slot], (((0,), (0,)), ((), ())), preferred_element_type=F32)

    def chunk(i, _):
        for k in range(KS):
            for s in reversed(range(len(OFFSETS))):
                if OFFSETS[s] % KS != k:
                    continue
                c = i - OFFSETS[s] // KS

                @pl.when((c >= 0) & (c < NC))
                def _():
                    stage(s, c)

            @pl.when(i < NC)
            def _():
                t = i * KS + k

                @pl.when(t + NG - 1 < NC * KS)
                def _():
                    g_copy(t + NG - 1).start()

                @pl.when(i % PER == 0)
                def _():
                    a_copy(0, k).wait()

                g_copy(t).wait()
                if k == 0:
                    acc[i % 2] = dot(k, t % NG)
                else:
                    acc[i % 2] += dot(k, t % NG)

                @pl.when(i == PER - 1)
                def _():
                    a_copy(1, k).start()
        return 0

    lax.fori_loop(0, NC + OFFSETS[-1] // KS + 0, chunk, 0)
    for gi in range(ng):
        for c in range(NC):
            out_copy(gi, c).wait()


def solution(mesh):
    ng = len(GROUPS)
    dma = pltpu.SemaphoreType.DMA
    scratch = [pltpu.VMEM((KS, TK, D), BF16), pltpu.VMEM((NG, TK, FC), BF16), pltpu.VMEM((2, D, FC), F32)]
    scratch += [pltpu.VMEM((2, 4, PR, w), F32) for _, w in GROUPS]
    scratch += [pltpu.VMEM((2, 16, PR, w), BF16) for _, w in GROUPS]
    scratch += [pltpu.VMEM((2, 16, PR, w), BF16) for _, w in GROUPS]
    scratch += [pltpu.VMEM((NC, 16, PR, w), BF16) for _, w in GROUPS]
    scratch += [dma((KS,)), dma((NG,)), dma((ng, 5, 2)), dma((ng, 5, 2)),
                dma((ng, 4, NC)), dma((ng, 4, NC)), dma((ng, NC))]

    def local(a, g):
        out = pl.pallas_call(
            kernel,
            out_shape=jax.ShapeDtypeStruct((MATS, 16, PR, FF), BF16),
            in_specs=[pl.BlockSpec(memory_space=pl.ANY)] * 2,
            out_specs=pl.BlockSpec(memory_space=pl.ANY),
            scratch_shapes=scratch,
            compiler_params=pltpu.CompilerParams(
                collective_id=0, has_side_effects=True, vmem_limit_bytes=63 * 2**20),
            name="summed_grads",
        )(a, g)
        return out.reshape(MATS, D, FF)

    spec = P(("rep", "dp"))
    return jax.shard_map(local, mesh=mesh, in_specs=(spec, spec), out_specs=P("rep"), check_vma=False)
```

time: 443 us -> 157 us (0.35)
  blocking collectives: 342 us -> 0 us
  Pallas kernels: 0 us -> 147 us
  matrix products: 101 us -> 0 us
  local copies, waits for them, and re-layouts: 0 us -> 9.71 us
    dot_general x1 -> x0, blocking collectives: 342 us -> none  [step(): jnp.einsum('rsntd,rsntf->rndf', a, g, preferred_element_type=jnp.float32)]
    pallas_call x0 -> x1, Pallas kernels: none -> 147 us  [local(): pl.pallas_call(kernel, out_shape=jax.ShapeDtypeStruct((MATS, 16, PR, FF),...]
    dot_general x1 -> x0, matrix products: 101 us -> none  [step(): jnp.einsum('rsntd,rsntf->rndf', a, g, preferred_element_type=jnp.float32)]
    unnamed x0 -> x1, local copies, waits for them, and re-layouts: none -> 9.71 us
where the time goes in v1:
time: 157 us
  Pallas kernels  147 us (94%)
  local copies, waits for them, and re-layouts  9.71 us (6%)
    pallas_call x1, Pallas kernels, local(): pl.pallas_call(kernel, out_shape=jax.ShapeDtypeStruct((MATS, 16, PR, FF),...  147 us
    unnamed x1, local copies, waits for them, and re-layouts  9.71 us

profile of v1, /device:TPU:0, one launch (start us, length us, event | category | flops | bytes accessed | tf_op | source)
XLA Modules:
  0.0 157.1 jit_solution(3841158757543211040)
XLA Ops:
  0.0 147.3 %summed_grads.1 = bf16[2,16,40,4096]{3,2,1,0:T(8,128)(2,1)} custom-call(bf16[1,2,8192,640]{3,2,1,0:T(8,128)(2,1)} %a_ref.1, bf16[1,2,8192,4096]{3,2,1,0:T(8,128)(2,1)} %g_ref.1), custom_call_target="tpu_custom_call" | custom-call | tf_op jit(solution)/shard_map/summed_grads/pallas_call | solution.py:189
  147.3 9.7 %copy.4 = bf16[2,640,4096]{2,1,0:T(8,128)(2,1)} copy(bf16[2,640,4096]{2,1,0:T(8,128)(2,1)} %bitcast.1) | data formatting | bytes 20971520

commit v2 on v0

v2 whole, which is shorter than its diff:
```python
import jax
import jax.numpy as jnp
from jax import lax
from jax.experimental import pallas as pl
from jax.experimental.pallas import tpu as pltpu
from jax.sharding import PartitionSpec as P

T, D, FF, MATS = 8192, 640, 4096, 2
FC = 512
TK = 4096
KS = T // TK
PAIRS = MATS * FF // FC // 2
HALF = PAIRS // MATS
LOOP = PAIRS - 1
NG = 3
NA = 4
PR = D // 16
F32, BF16 = jnp.float32, jnp.bfloat16


class Plan:
    def __init__(self, groups, width, count, slots):
        self.groups, self.width, self.count, self.slots = groups, width, count, slots
        self.q = len(groups)
        self.n = [16]
        for g in groups:
            self.n.append(self.n[-1] >> len(g))
        self.lo, self.sem, at, sem = [], [], 0, 0
        for j, g in enumerate(groups):
            self.lo.append(at)
            self.sem.append(sem)
            at += ((1 << len(g)) - 1) * self.n[j + 1]
            sem += (1 << len(g)) - 1
        self.last, self.sems = at, sem
        self.stages = 2 * self.q + 2


PLANS = (
    Plan((("c",), ("x",), ("y", "w")), 512, LOOP, 2),
    Plan((("c",), ("y",), ("x", "w")), 512, LOOP, 2),
    Plan((("c",), ("x",), ("y", "w")), 512, 1, 1),
    Plan((("c",), ("y",), ("x", "w")), 256, 1, 1),
    Plan((("c",), ("x", "y", "w")), 256, 1, 1),
)
OFFSETS = ((0, 1, 3, 7, 9, 11, 13, 14), (0, 2, 4, 6, 9, 12, 14, 15))
DOT = None
ENDING = (
    (1, 0, 6), (1, 2, 5), (0, 3, 5), (1, 4, 4), (1, 5, 3), (0, 7, 3), DOT, (1, 1, 6), (0, 2, 6), (0, 5, 4), DOT,
    (2, 0, 0), (1, 3, 5), (0, 4, 5), (1, 5, 4), (2, 1, 0), (1, 6, 3), DOT, (3, 0, 0), (3, 1, 0), (1, 2, 6),
    (0, 3, 6), (1, 4, 5), (0, 6, 4), (1, 7, 3), DOT, (4, 0, 0), (2, 2, 0), (4, 1, 0), (1, 3, 6), (0, 4, 6),
    (0, 5, 5), (1, 6, 4), (0, 7, 4), (1, 7, 4), (3, 2, 0), (1, 5, 5), (2, 3, 0), (4, 2, 0), (1, 4, 6), (0, 6, 5),
    (0, 7, 5), (0, 5, 6), (3, 3, 0), (2, 4, 0), (4, 3, 0), (1, 6, 5), (1, 7, 5), (3, 4, 0), (1, 5, 6), (0, 6, 6),
    (2, 5, 0), (0, 7, 6), (4, 4, 0), (3, 5, 0), (4, 5, 0), (1, 6, 6), (2, 6, 0), (3, 6, 0), (1, 7, 6), (2, 7, 0),
    (3, 7, 0),
)
NP = len(PLANS)


def kernel(a_ref, g_ref, *rest):
    done, (ab, gb, acc), rest = rest[:NP], rest[NP:NP + 3], rest[NP + 3:]
    part, send, recv, rs_s, rs_r, ag_s, ag_r = (rest[i * NP:(i + 1) * NP] for i in range(7))
    asem, gsem = rest[7 * NP:]
    me = lax.axis_index("dp")
    bits = {"x": me // 16, "y": (me // 8) % 2, "h": (me // 4) % 2, "w": (me // 2) % 2, "c": me % 2}
    size = {"x": 16, "y": 8, "h": 4, "w": 2, "c": 1}

    def a_copy(n, k):
        rows = pl.ds(k * TK, TK)
        return pltpu.make_async_copy(a_ref.at[0, n, rows, :], ab.at[rows, :], asem.at[k])

    def g_copy(t):
        c, k = t // KS, t % KS
        rows = pl.ds(pl.multiple_of(k * TK, TK), TK)
        cols = pl.ds(pl.multiple_of((c % (2 * HALF)) * FC, FC), FC)
        return pltpu.make_async_copy(g_ref.at[0, c // (2 * HALF), rows, cols], gb.at[t % NG], gsem.at[t % NG])

    for k in range(KS):
        a_copy(0, k).start()
        g_copy(jnp.int32(k)).start()

    def flip(dims, m):
        value = 0
        for i, d in enumerate(dims):
            one = (m >> (len(dims) - 1 - i)) & 1
            value = value * 2 + (1 - bits[d] if one else bits[d])
        return value

    def peer(dims, m):
        to = me
        for i, d in enumerate(dims):
            if (m >> (len(dims) - 1 - i)) & 1:
                to = to + size[d] * (1 - 2 * bits[d])
        return (0, to)

    barrier = pltpu.get_barrier_semaphore()
    cube = ("x", "y", "w")
    partners = [peer(("c",), 1), peer(("h",), 1)] + [peer(cube, m) for m in range(1, 8)]
    for to in partners:
        pl.semaphore_signal(barrier, inc=1, device_id=to, device_id_type=pl.DeviceIdType.MESH)
    pl.semaphore_wait(barrier, len(partners))

    def remote(src, dst, ssem, rsem, to):
        return pltpu.make_async_remote_copy(
            src_ref=src, dst_ref=dst, send_sem=ssem, recv_sem=rsem,
            device_id=to, device_id_type=pl.DeviceIdType.MESH)

    def masks(plan, j):
        return range(1, 1 << len(plan.groups[j]))

    def rs_copy(pi, j, m, slot):
        plan = PLANS[pi]
        if j == plan.q:
            where, sem, to = pl.ds(plan.last, 1), plan.sems, peer(("h",), 1)
        else:
            n = plan.n[j + 1]
            where, sem, to = pl.ds(plan.lo[j] + (m - 1) * n, n), plan.sem[j] + m - 1, peer(plan.groups[j], m)
        return remote(send[pi].at[slot, where], recv[pi].at[slot, where],
                      rs_s[pi].at[sem, slot], rs_r[pi].at[sem, slot], to)

    def ag_copy(pi, j, m, c):
        plan = PLANS[pi]
        first = 0
        for i in range(j + 1):
            first = first + flip(plan.groups[i], 0) * plan.n[i + 1]
        where, sem = pl.ds(first, plan.n[j + 1]), plan.sem[j] + m - 1
        return remote(done[pi].at[c, where], done[pi].at[c, where],
                      ag_s[pi].at[sem, c], ag_r[pi].at[sem, c], peer(plan.groups[j], m))

    def stage(pi, s, c, tot):
        plan = PLANS[pi]
        q, w, slot = plan.q, plan.width, c % plan.slots

        def total(piece):
            return acc[tot, pl.ds(pl.multiple_of(piece * PR, 8), PR), :w]

        def value(p):
            v = total(flip(plan.groups[0], 0) * plan.n[1] + p) if s == 1 else part[pi][slot, p]
            for m in masks(plan, s - 1):
                v = v + recv[pi][slot, plan.lo[s - 1] + (m - 1) * plan.n[s] + p].astype(F32)
            return v

        if 1 <= s <= q:
            for m in masks(plan, s - 1):
                rs_copy(pi, s - 1, m, slot).wait()
        if s < q:
            n = plan.n[s + 1]
            for m in masks(plan, s):
                give = flip(plan.groups[s], m) * n
                for j in range(n):
                    v = total(give + j) if s == 0 else value(give + j)
                    send[pi][slot, plan.lo[s] + (m - 1) * n + j] = v.astype(BF16)
                rs_copy(pi, s, m, slot).start()
            if s > 0:
                keep = flip(plan.groups[s], 0) * n
                for j in range(n):
                    part[pi][slot, j] = value(keep + j)
        elif s == q:
            send[pi][slot, plan.last] = value(0).astype(BF16)
            rs_copy(pi, q, 0, slot).start()
        elif s == q + 1:
            rs_copy(pi, q, 0, slot).wait()
            mine = 0
            for i in range(q):
                mine = mine + flip(plan.groups[i], 0) * plan.n[i + 1]
            both = send[pi][slot, plan.last].astype(F32) + recv[pi][slot, plan.last].astype(F32)
            done[pi][c, mine] = both.astype(BF16)
        else:
            j = 2 * q + 1 - s
            for m in masks(plan, j):
                ag_copy(pi, j, m, c).wait()

    def gather(pi, s, c):
        plan = PLANS[pi]
        j = 2 * plan.q - s
        if 0 <= j < plan.q:
            for m in masks(plan, j):
                ag_copy(pi, j, m, c).start()

    def run(pi, s, c, tot):
        stage(pi, s, c, tot)
        if s > PLANS[pi].q:
            gather(pi, s, c)

    def dot(k, slot, cols):
        rows = slice(k * TK, (k + 1) * TK)
        return lax.dot_general(ab[rows, :], gb[slot, :, cols], (((0,), (0,)), ((), ())), preferred_element_type=F32)

    every = slice(0, FC)

    def pair(i, _):
        for u in range(2 * KS):
            which, k = u // KS, u % KS
            stages = [(OFFSETS[pi][s], pi, s) for pi in range(2) for s in range(PLANS[pi].stages)]
            for off, pi, s in sorted(stages, key=lambda v: (-v[0], v[1])):
                e = (pi + 1) * KS + off
                if e % (2 * KS) != u:
                    continue
                c = i - e // (2 * KS)

                @pl.when(c >= 0)
                def _():
                    run(pi, s, c, (2 * c + pi) % NA)

            t = i * 2 * KS + u
            g_copy(t + NG - 1).start()
            if which == 0:
                @pl.when(i % HALF == 0)
                def _():
                    a_copy(0, k).wait()

            g_copy(t).wait()
            tot = (2 * i + which) % NA
            if k == 0:
                acc[tot] = dot(k, t % NG, every)
            else:
                acc[tot] += dot(k, t % NG, every)
            if which == 1:
                @pl.when(i == HALF - 1)
                def _():
                    a_copy(1, k).start()
        return 0

    lax.fori_loop(0, LOOP, pair, 0)

    base = 2 * LOOP
    t0 = base * KS

    def tail_dot(step):
        if step < KS:
            if t0 + step + NG - 1 < 2 * PAIRS * KS:
                g_copy(jnp.int32(t0 + step + NG - 1)).start()
            g_copy(jnp.int32(t0 + step)).wait()
            d = dot(step, (t0 + step) % NG, every)
            if step == 0:
                acc[base % NA] = d
            else:
                acc[base % NA] += d
        else:
            part_of = step - KS
            cols = slice(part_of * 256, part_of * 256 + 256)
            for k in range(KS):
                if part_of == 0:
                    if t0 + KS + k + NG - 1 < 2 * PAIRS * KS:
                        g_copy(jnp.int32(t0 + KS + k + NG - 1)).start()
                    g_copy(jnp.int32(t0 + KS + k)).wait()
            tot = (base + 1 + part_of) % NA
            acc[tot, :, :256] = dot(0, (t0 + KS) % NG, cols) + dot(1, (t0 + KS + 1) % NG, cols)

    step = 0
    for item in ENDING:
        if item is DOT:
            tail_dot(step)
            step += 1
        else:
            pi, s, c = item
            run(pi, s, c, (2 * c + pi if pi < 2 else base + pi - 2) % NA)


def write_out(*refs):
    done, o_ref, sem = refs[:NP], refs[NP], refs[NP + 1]
    copies = []

    def copy(pi, c, at):
        w, per = PLANS[pi].width, FF
        cols = pl.ds(at % per, w)
        copies.append(pltpu.make_async_copy(
            done[pi].at[c], o_ref.at[at // per, :, :, cols], sem.at[len(copies)]))

    for c in range(LOOP):
        for pi in range(2):
            copy(pi, c, (2 * c + pi) * FC)
    at = 2 * LOOP * FC
    for pi in range(2, NP):
        copy(pi, 0, at)
        at += PLANS[pi].width
    for one in copies:
        one.start()
    for one in copies:
        one.wait()


def solution(mesh):
    dma = pltpu.SemaphoreType.DMA
    scratch = [pltpu.VMEM((T, D), BF16), pltpu.VMEM((NG, TK, FC), BF16), pltpu.VMEM((NA, D, FC), F32)]
    scratch += [pltpu.VMEM((p.slots, max(p.n[2], 1), PR, p.width), F32) for p in PLANS]
    scratch += [pltpu.VMEM((p.slots, 16, PR, p.width), BF16) for p in PLANS] * 2
    scratch += [dma((p.sems + 1, p.slots)) for p in PLANS] * 2
    scratch += [dma((p.sems, p.count)) for p in PLANS] * 2
    scratch += [dma((KS,)), dma((NG,))]
    shapes = [(p.count, 16, PR, p.width) for p in PLANS]

    def local(a, g):
        done = pl.pallas_call(
            kernel,
            out_shape=[pltpu.VMEM(s, BF16) for s in shapes],
            in_specs=[pl.BlockSpec(memory_space=pl.ANY)] * 2,
            out_specs=[pl.BlockSpec(memory_space=pltpu.VMEM)] * NP,
            scratch_shapes=scratch,
            compiler_params=pltpu.CompilerParams(
                collective_id=0, has_side_effects=True, vmem_limit_bytes=50 * 2**20),
            name="summed_grads",
        )(a, g)
        done = [pltpu.with_memory_space_constraint(d, pltpu.VMEM) for d in done]
        out = pl.pallas_call(
            write_out,
            out_shape=jax.ShapeDtypeStruct((MATS, 16, PR, FF), BF16),
            in_specs=[pl.BlockSpec(memory_space=pltpu.VMEM)] * NP,
            out_specs=pl.BlockSpec(memory_space=pl.ANY),
            scratch_shapes=[dma((2 * LOOP + 3,))],
            compiler_params=pltpu.CompilerParams(vmem_limit_bytes=2**20),
            name="write_out",
        )(*done)
        return out.reshape(MATS, D, FF)

    spec = P(("rep", "dp"))
    return jax.shard_map(local, mesh=mesh, in_specs=(spec, spec), out_specs=P("rep"), check_vma=False)
```

time: 443 us -> 143 us (0.32)
  blocking collectives: 342 us -> 0 us
  Pallas kernels: 0 us -> 142 us
  matrix products: 101 us -> 0 us
    dot_general x1 -> x0, blocking collectives: 342 us -> none  [step(): jnp.einsum('rsntd,rsntf->rndf', a, g, preferred_element_type=jnp.float32)]
    pallas_call x0 -> x2, Pallas kernels: none -> 142 us  [the longest x1 138 us: local(): pl.pallas_call(kernel, out_shape=[pltpu.VMEM(s, BF16) for s in shapes], i...]
    dot_general x1 -> x0, matrix products: 101 us -> none  [step(): jnp.einsum('rsntd,rsntf->rndf', a, g, preferred_element_type=jnp.float32)]
where the time goes in v2:
time: 143 us; the launch traced here: 142 us
  Pallas kernels  142 us (99%)
    pallas_call x1, Pallas kernels, local(): pl.pallas_call(kernel, out_shape=[pltpu.VMEM(s, BF16) for s in shapes], i...  138 us
    pallas_call x1, Pallas kernels, local(): pl.pallas_call(write_out, out_shape=jax.ShapeDtypeStruct((MATS, 16, PR, F...  4.06 us

profile of v2, /device:TPU:0, one launch (start us, length us, event | category | flops | bytes accessed | tf_op | source)
XLA Modules:
  0.0 142.4 jit_solution(7116265129315196725)
XLA Ops:
  0.0 138.2 %summed_grads.1 = (bf16[7,16,40,512]{3,2,1,0:T(8,128)(2,1)S(1)}, bf16[7,16,40,512]{3,2,1,0:T(8,128)(2,1)S(1)}, bf16[1,16,40,512]{3,2,1,0:T(8,128)(2,1)S(1)}, bf1...) custom-call(bf16[1,2,8192,640]{3,2,1,0:T(8,128)(2,1)} %a_ref.1, bf16[1,2,8192,4096]{3,2,1,0:T(8,128)(2,1)} %g_ref.1), custom_call_target="tpu_custom_call" | custom-call | tf_op jit(solution)/shard_map/summed_grads/pallas_call | solution.py:293
  138.2 4.1 %write_out.1 = bf16[2,16,40,4096]{3,2,1,0:T(8,128)(2,1)} custom-call(bf16[7,16,40,512]{3,2,1,0:T(8,128)(2,1)S(1)} %get-tuple-element.10.refs_0_, bf16[7,16,40,512]{3,2,1,0:T(8,128)(2,1)S(1)} %get-tuple-element.11.refs_1_, bf16[1,16,40,512]{3,2,1,0:T(8,128)(2,1)S(1)} %get-tuple-element.12.refs_2_, bf16[1,16,40,256]{3,2,1,0:T(8,128)(2,1)S(1)} %get-tuple-element.13.refs_3_, ...), custom_call_target="tpu_custom_call" | custom-call | tf_op jit(solution)/shard_map/write_out/pallas_call | solution.py:304

commit v3 on v2

--- a/solution.py
+++ b/solution.py
@@ -42,7 +42,7 @@
     Plan((("c",), ("y",), ("x", "w")), 256, 1, 1),
     Plan((("c",), ("x", "y", "w")), 256, 1, 1),
 )
-OFFSETS = ((0, 1, 3, 7, 9, 11, 13, 14), (0, 2, 4, 6, 9, 12, 14, 15))
+OFFSETS = ((0, 1, 3, 6, 9, 11, 13, 16), (0, 2, 4, 6, 10, 12, 14, 15))
 DOT = None
 ENDING = (
     (1, 0, 6), (1, 2, 5), (0, 3, 5), (1, 4, 4), (1, 5, 3), (0, 7, 3), DOT, (1, 1, 6), (0, 2, 6), (0, 5, 4), DOT,

time: 143 us -> 142 us (level)
  no operation moved by 1% of the time
where the time goes in v3:
time: 142 us
  Pallas kernels  142 us (100%)
    pallas_call x1, Pallas kernels, local(): pl.pallas_call(kernel, out_shape=[pltpu.VMEM(s, BF16) for s in shapes], i...  138 us
    pallas_call x1, Pallas kernels, local(): pl.pallas_call(write_out, out_shape=jax.ShapeDtypeStruct((MATS, 16, PR, F...  4.06 us

profile of v3, /device:TPU:0, one launch (start us, length us, event | category | flops | bytes accessed | tf_op | source)
XLA Modules:
  0.0 141.8 jit_solution(14204179024711305312)
XLA Ops:
  0.0 137.6 %summed_grads.1 = (bf16[7,16,40,512]{3,2,1,0:T(8,128)(2,1)S(1)}, bf16[7,16,40,512]{3,2,1,0:T(8,128)(2,1)S(1)}, bf16[1,16,40,512]{3,2,1,0:T(8,128)(2,1)S(1)}, bf1...) custom-call(bf16[1,2,8192,640]{3,2,1,0:T(8,128)(2,1)} %a_ref.1, bf16[1,2,8192,4096]{3,2,1,0:T(8,128)(2,1)} %g_ref.1), custom_call_target="tpu_custom_call" | custom-call | tf_op jit(solution)/shard_map/summed_grads/pallas_call | solution.py:293
  137.6 4.1 %write_out.1 = bf16[2,16,40,4096]{3,2,1,0:T(8,128)(2,1)} custom-call(bf16[7,16,40,512]{3,2,1,0:T(8,128)(2,1)S(1)} %get-tuple-element.10.refs_0_, bf16[7,16,40,512]{3,2,1,0:T(8,128)(2,1)S(1)} %get-tuple-element.11.refs_1_, bf16[1,16,40,512]{3,2,1,0:T(8,128)(2,1)S(1)} %get-tuple-element.12.refs_2_, bf16[1,16,40,256]{3,2,1,0:T(8,128)(2,1)S(1)} %get-tuple-element.13.refs_3_, ...), custom_call_target="tpu_custom_call" | custom-call | tf_op jit(solution)/shard_map/write_out/pallas_call | solution.py:304
